TPU v7x, 32 devices: a whole 2x2x4 slice. The times are simulated.
32 devices in a mesh: row: 4 (over y, x), col: 4 (over z), fiber: 2 (over core).
Axes of the slice: x: 2, y: 2, z: 4, core: 2. Of those that a mesh axis runs over, the one named last changes fastest.
Arguments:
- user_factors: float32 [8192, 128], P(('row', 'col', 'fiber')), may hold values from -3 to 3
- item_factors: bfloat16 [16384, 128], P(('row', 'col')), may hold values from -0.119628906 to 0.119628906
- ratings: bfloat16 [4, 4, 256, 128, 128], P('row', 'col', 'fiber'), may hold values from -2 to 2, as said below
- block_user: int32 [4, 4, 256], P('row', 'col', 'fiber'), may hold values from 0 to 15, as said below
- block_item: int32 [4, 4, 256], P('row', 'col', 'fiber'), may hold values from 0 to 31, as said below
- counts: int32 [8192], P(('row', 'col', 'fiber')), may hold values from 1 to 8192, as said below
Outputs:
- factors: float32 [8192, 128], P(('row', 'col', 'fiber'))
- residual: float32 [8192, 128], P(('row', 'col', 'fiber'))
Inputs may be any that keep to these rules, and one draw needn't show every extreme that they name: `block_user`: within one tile (one row index and one column index) the occupied blocks are distinct; each user block index appears in exactly 16 blocks of every tile, which fall on the two fiber halves at random. `block_item`: an item block index within the column slab. counts[u] equals the number of nonzero entries of ratings that belong to user u, over all blocks; some user has every rating of its blocks observed. Every user row of every occupied block has an observed rating; observed ratings have magnitude 0.25 or more.
All inputs are finite; a program needn't handle non-finite values.
Results may differ from a plain program's by a relative error of at most 0.012.
The roundings to bfloat16 on the way count: a program that leaves them out, or rounds other values in their place, can miss the bound.
Values may be sent and summed in bfloat16 or wider, within the bound.
A program may use at most 64 MiB of HBM per device.

v0:
```python
import functools

import jax
import jax.numpy as jnp
from jax import lax
from jax.experimental import pallas as pl
from jax.experimental.pallas import tpu as pltpu
from jax.sharding import PartitionSpec as P

ITERS = 2

reg_weight = 0.0004
tiny = 1e-06

MESH = pl.DeviceIdType.MESH


def sweep_kernel(
    sizes, pos_ref, item_ref, uf_hbm, counts_hbm, items_hbm, ratings_hbm, x_ref, r_ref,
    vbuf, rbuf, pbuf, part, recv, p_ref, damp_ref, counts_ref,
    user_sem, count_sem, item_sem, rating_sem, v_send, v_recv, d_send, d_recv, t_send, t_recv, g_send, g_recv, s_send, s_recv,
):
    rows, cols, fibers = sizes
    my_row, my_col, my_fiber = lax.axis_index("row"), lax.axis_index("col"), lax.axis_index("fiber")
    held_items = items_hbm.shape[0]
    share = held_items // fibers
    held_blocks, block = ratings_hbm.shape[0], ratings_hbm.shape[1]
    own_users = uf_hbm.shape[0] // block
    per_user = pos_ref.shape[0] // (cols * own_users)

    def row_of(d):
        return lax.rem(my_row + d, rows)

    def col_of(d):
        col, bit = my_col, 1
        while bit <= d:
            if d & bit:
                col = col + bit * (1 - 2 * lax.rem(lax.div(my_col, bit), 2))
            bit *= 2
        return col

    def fiber_of(d):
        return lax.rem(my_fiber + d, fibers)

    user_load = pltpu.make_async_copy(uf_hbm, x_ref, user_sem)
    user_load.start()
    count_load = pltpu.make_async_copy(counts_hbm, counts_ref, count_sem)
    count_load.start()
    own_items = pl.ds(my_row * held_items, held_items)
    item_load = pltpu.make_async_copy(items_hbm, vbuf.at[own_items], item_sem)
    item_load.start()
    own_ratings = pl.ds(my_fiber * held_blocks, held_blocks)
    rating_load = pltpu.make_async_copy(ratings_hbm, rbuf.at[own_ratings], rating_sem)
    rating_load.start()

    barrier = pltpu.get_barrier_semaphore()
    for d in range(1, rows):
        pl.semaphore_signal(barrier, inc=1, device_id={"row": row_of(d)}, device_id_type=MESH)
    for d in range(1, cols):
        pl.semaphore_signal(barrier, inc=1, device_id={"col": col_of(d)}, device_id_type=MESH)
    for d in range(1, fibers):
        pl.semaphore_signal(barrier, inc=1, device_id={"fiber": fiber_of(d)}, device_id_type=MESH)

    user_load.wait()
    for j in range(own_users):
        pbuf[0, my_col, j] = x_ref[pl.ds(j * block, block), :].astype(jnp.bfloat16)
    pl.semaphore_wait(barrier, rows + cols + fibers - 3)

    def gather_copy(stage, d, j):
        return pltpu.make_async_remote_copy(
            src_ref=pbuf.at[stage, my_col, j],
            dst_ref=pbuf.at[stage, my_col, j],
            send_sem=g_send.at[stage, d, j],
            recv_sem=g_recv.at[stage, d, j],
            device_id={"col": col_of(d)},
            device_id_type=MESH,
        )

    def scatter_copy(stage, d, j):
        return pltpu.make_async_remote_copy(
            src_ref=part.at[stage, d, j],
            dst_ref=recv.at[stage, d, j],
            send_sem=s_send.at[stage, d, j],
            recv_sem=s_recv.at[stage, d, j],
            device_id={"col": col_of(d & -d)},
            device_id_type=MESH,
        )

    item_sends = []
    for d in range(1, rows):
        copy = pltpu.make_async_remote_copy(
            src_ref=items_hbm.at[pl.ds(my_fiber * share, share)],
            dst_ref=vbuf.at[pl.ds(my_row * held_items + my_fiber * share, share)],
            send_sem=v_send.at[d],
            recv_sem=v_recv.at[d],
            device_id={"row": row_of(d)},
            device_id_type=MESH,
        )
        copy.start()
        item_sends.append(copy)
    order = sorted(range(1, cols), key=lambda d: (d & -d, -d))
    for j in range(own_users):
        for d in order:
            gather_copy(0, d, j).start()
    rating_sends = []
    for e in range(1, fibers):
        copy = pltpu.make_async_remote_copy(
            src_ref=ratings_hbm,
            dst_ref=rbuf.at[own_ratings],
            send_sem=t_send.at[e],
            recv_sem=t_recv.at[e],
            device_id={"fiber": fiber_of(e)},
            device_id_type=MESH,
        )
        copy.start()
        rating_sends.append(copy)
    shared = []
    for d in range(1, rows):
        item_sends[d - 1].wait_recv()
        source = lax.rem(my_row + rows - d, rows)
        piece = pl.ds(source * held_items + my_fiber * share, share)
        for e in range(1, fibers):
            copy = pltpu.make_async_remote_copy(
                src_ref=vbuf.at[piece],
                dst_ref=vbuf.at[piece],
                send_sem=d_send.at[d, e],
                recv_sem=d_recv.at[d, e],
                device_id={"fiber": fiber_of(e)},
                device_id_type=MESH,
            )
            copy.start()
            shared.append(copy)
    count_load.wait()
    for j in range(own_users):
        scaled = reg_weight * counts_ref[pl.ds(j, 1), :].astype(jnp.float32)
        across = jnp.broadcast_to(scaled, (block, block))
        damp_ref[pl.ds(j * block, block), :] = jnp.broadcast_to(
            jnp.transpose(across)[:, :1], (block, damp_ref.shape[1])
        )
    item_load.wait()
    rating_load.wait()
    for copy in rating_sends + shared:
        copy.wait_recv()

    def user_terms(stage, col, j):
        rows_of_user = pbuf[stage, col, j]
        base = (col * own_users + j) * per_user

        items = jnp.concatenate([vbuf[item_ref[base + i]] for i in range(per_user)], axis=0)
        ratings = jnp.concatenate([rbuf[pos_ref[base + i]] for i in range(per_user)], axis=1)
        predicted = lax.dot_general(
            rows_of_user, items, (((1,), (1,)), ((), ())), preferred_element_type=jnp.float32
        )
        ratings = ratings.astype(jnp.float32)
        if stage == 0:
            weights = jnp.where(ratings != 0, ratings - predicted, 0.0)
        else:
            weights = jnp.where(ratings != 0, predicted, 0.0)
        return jnp.dot(weights.astype(jnp.bfloat16), items, preferred_element_type=jnp.float32)

    def add_received(stage, d, j):
        total = part[stage, d, j]
        bit = 1
        while bit < (d & -d if d else cols):
            scatter_copy(stage, d | bit, j).wait_recv()
            total = total + recv[stage, d | bit, j]
            bit *= 2
        return total

    def scatter(stage):
        for j in range(own_users):
            for d in [0] + order:
                if d:
                    gather_copy(stage, d, j).wait_recv()
                part[stage, d, j] = user_terms(stage, col_of(d), j)
                if d & 1:
                    scatter_copy(stage, d, j).start()
        for d in order:
            if d & 1 == 0:
                for j in range(own_users):
                    part[stage, d, j] = add_received(stage, d, j)
                    scatter_copy(stage, d, j).start()

    def begin(stage, j, direction):
        users = pl.ds(j * block, block)
        p_ref[users, :] = direction
        pbuf[stage, my_col, j] = direction.astype(jnp.bfloat16)
        for d in order:
            gather_copy(stage, d, j).start()

    scatter(0)
    squares = []
    for j in range(own_users):
        users = pl.ds(j * block, block)
        residual = add_received(0, 0, j) - damp_ref[users, :] * x_ref[users, :]
        begin(1, j, residual)
        r_ref[users, :] = residual
        squares.append(jnp.sum(residual * residual, axis=1, keepdims=True))
    for iteration in range(ITERS):
        scatter(iteration + 1)
        for j in range(own_users):
            users = pl.ds(j * block, block)
            direction = p_ref[users, :]
            image = add_received(iteration + 1, 0, j) + damp_ref[users, :] * direction
            step_size = squares[j] / (jnp.sum(direction * image, axis=1, keepdims=True) + tiny)
            residual = r_ref[users, :] - step_size * image
            if iteration + 1 < ITERS:
                renewed = jnp.sum(residual * residual, axis=1, keepdims=True)
                begin(iteration + 2, j, residual + renewed / (squares[j] + tiny) * direction)
                squares[j] = renewed
            r_ref[users, :] = residual
            x_ref[users, :] = x_ref[users, :] + step_size * direction

    for copy in item_sends + rating_sends + shared:
        copy.wait_send()
    for stage in range(ITERS + 1):
        for d in range(1, cols):
            for j in range(own_users):
                gather_copy(stage, d, j).wait_send()
                scatter_copy(stage, d, j).wait_send()


def per_device(sizes, slab_users, user_factors, item_factors, ratings, block_user, block_item, counts):
    rows, cols, fibers = sizes
    held_blocks, block = ratings.shape[2], ratings.shape[3]
    rank = user_factors.shape[1]
    users = user_factors.shape[0]
    own_users = users // block
    item_blocks = item_factors.shape[0] // block
    per_user = fibers * held_blocks // (slab_users // block)

    both = lax.all_gather(jnp.stack([block_user[0, 0], block_item[0, 0]]), "fiber", axis=0)
    owners = both[:, 0].reshape(-1)
    columns = both[:, 1].reshape(-1)
    here = jnp.arange(owners.shape[0], dtype=jnp.int32)
    keys = owners * owners.shape[0] + here
    ranks = jnp.sum((keys[None, :] < keys[:, None]).astype(jnp.int32), axis=1)
    groups = jnp.arange(cols, dtype=jnp.int32)[:, None] * fibers + lax.axis_index("fiber")
    wanted = (
        groups[:, :, None] * (own_users * per_user)
        + jnp.arange(own_users * per_user, dtype=jnp.int32)[None, None, :]
    ).reshape(-1)
    match = wanted[:, None] == ranks[None, :]
    positions = jnp.sum(jnp.where(match, here[None, :], 0), axis=1)
    items = jnp.sum(jnp.where(match, columns[None, :], 0), axis=1)

    stages = ITERS + 1
    dma = pltpu.SemaphoreType.DMA
    vmem = pl.BlockSpec(memory_space=pltpu.VMEM)
    smem = pl.BlockSpec(memory_space=pltpu.SMEM)
    hbm = pl.BlockSpec(memory_space=pl.ANY)
    return pl.pallas_call(
        functools.partial(sweep_kernel, sizes),
        out_shape=(
            jax.ShapeDtypeStruct((users, rank), jnp.float32),
            jax.ShapeDtypeStruct((users, rank), jnp.float32),
        ),
        in_specs=[smem, smem, hbm, hbm, hbm, hbm],
        out_specs=(vmem, vmem),
        scratch_shapes=[
            pltpu.VMEM((rows * item_blocks, block, rank), jnp.bfloat16),
            pltpu.VMEM((fibers * held_blocks, block, block), jnp.bfloat16),
            pltpu.VMEM((stages, cols, own_users, block, rank), jnp.bfloat16),
            pltpu.VMEM((stages, cols, own_users, block, rank), jnp.float32),
            pltpu.VMEM((stages, cols, own_users, block, rank), jnp.float32),
            pltpu.VMEM((users, rank), jnp.float32),
            pltpu.VMEM((users, rank), jnp.float32),
            pltpu.VMEM((own_users, block), jnp.int32),
            dma,
            dma,
            dma,
            dma,
            dma((rows,)),
            dma((rows,)),
            dma((rows, fibers)),
            dma((rows, fibers)),
            dma((fibers,)),
            dma((fibers,)),
            dma((stages, cols, own_users)),
            dma((stages, cols, own_users)),
            dma((stages, cols, own_users)),
            dma((stages, cols, own_users)),
        ],
        compiler_params=pltpu.CompilerParams(
            collective_id=0, has_side_effects=True, vmem_limit_bytes=67043328
        ),
    )(
        positions,
        items,
        user_factors,
        counts.reshape(own_users, block),
        item_factors.reshape(item_blocks, block, rank),
        ratings[0, 0],
    )


def solution(mesh):
    sizes = (mesh.shape["row"], mesh.shape["col"], mesh.shape["fiber"])

    def whole(user_factors, item_factors, ratings, block_user, block_item, counts):
        slab_users = user_factors.shape[0] // sizes[0]
        return jax.shard_map(
            functools.partial(per_device, sizes, slab_users),
            mesh=mesh,
            in_specs=(
                P(("row", "col", "fiber"), None),
                P(("row", "col"), None),
                P("row", "col", "fiber", None, None),
                P("row", "col", "fiber"),
                P("row", "col", "fiber"),
                P(("row", "col", "fiber")),
            ),
            out_specs=(P(("row", "col", "fiber"), None), P(("row", "col", "fiber"), None)),
            check_vma=False,
        )(user_factors, item_factors, ratings, block_user, block_item, counts)

    return whole
```

profile of v0, /device:TPU:0, one launch (start us, length us, event | category | flops | bytes accessed | tf_op | source)
XLA Modules:
  0.0 67.8 jit_solution(14515146872938587684)
XLA Ops:
  0.6 0.7 %add_bitcast_fusion = s32[1,2,128]{2,1,0:T(2,128)S(1)} fusion(s32[1,128]{1,0:T(1,128)} %bitcast.16, s32[1,128]{1,0:T(1,128)} %bitcast.17), kind=kLoop, calls=%fused_computation.7 | loop fusion | flops 256 | bytes 2048
  1.3 1.9 %all-gather.1 = s32[2,2,128]{2,1,0:T(2,128)S(1)} all-gather(s32[1,2,128]{2,1,0:T(2,128)S(1)} %add_bitcast_fusion), channel_id=2, replica_groups=mesh['row'=4,'col'=4,'fiber'=2] {'fiber'}, dimensions={0}, use_global_device_ids=true | all-gather | bytes 3072 | tf_op jit(solution)/shard_map/all_gather | solution.py:232
  3.3 0.2 convert_reduce_fusion
  3.5 0.1 iota_add_fusion
  3.5 0.1 add.51
  3.6 0.7 %fusion.1 = (s32[128]{0:T(128)}, s32[128]{0:T(128)}) fusion(s32[256]{0:T(256)S(1)} %bitcast.13, s32[256]{0:T(256)S(1)} %convert_reduce_fusion, s32[128]{0:T(128)S(1)} %add.51), kind=kLoop, calls=%fused_computation.4 | loop fusion | flops 163584 | bytes 3584 | tf_op jit(solution)/shard_map/reduce_sum | solution.py:245
  4.3 60.3 %shard_map.77 = (f32[256,128]{1,0:T(8,128)}, f32[256,128]{1,0:T(8,128)}) custom-call(s32[128]{0:T(128)} %get-tuple-element.3.pos_ref, s32[128]{0:T(128)} %get-tuple-element.2.item_ref, f32[256,128]{1,0:T(8,128)} %uf_hbm.1, s32[2,128]{1,0:T(2,128)} %bitcast.15, bf16[8,128,128]{2,1,0:T(8,128)(2,1)} %bitcast.12, bf16[128,128,128]{2,1,0:T(8,128)(2,1)} %bitcast.11), custom_call_target="tpu_custom_call" | custom-call | tf_op jit(solution)/shard_map/pallas_call | solution.py:252
  64.6 1.6 %copy.10 = f32[256,128]{1,0:T(8,128)} copy(f32[256,128]{1,0:T(8,128)} %get-tuple-element.8) | data formatting | bytes 262144
  66.2 1.6 %copy.11 = f32[256,128]{1,0:T(8,128)} copy(f32[256,128]{1,0:T(8,128)} %get-tuple-element.9) | data formatting | bytes 262144
  (3 shorter events, 0.0 us)
where the time goes:
time: 68 us; the launch traced here: 67.8 us
  Pallas kernels  60.3 us (89%)
  local copies, waits for them, and re-layouts  3.22 us (5%)
  blocking collectives  1.95 us (3%)
  other arithmetic  1.66 us (2%)
    pallas_call x1, Pallas kernels, per_device(): pl.pallas_call(functools.partial(sweep_kernel, sizes), out_shape=(jax.Sha...  60.3 us
    unnamed x2, local copies, waits for them, and re-layouts  3.14 us
    all_gather x1, blocking collectives, per_device(): lax.all_gather(jnp.stack([block_user[0, 0], block_item[0, 0]]), 'fiber',...  1.95 us

commit v1 on v0

v1 whole, which is shorter than its diff:
```python
import functools

import jax
import jax.numpy as jnp
from jax import lax
from jax.experimental import pallas as pl
from jax.experimental.pallas import tpu as pltpu
from jax.sharding import PartitionSpec as P

ITERS = 2
CHUNKS = 4

reg_weight = 0.0004
tiny = 1e-06

top = 32700.0
steps = 128.0
floor = 2.0**-100
pad = 16

MESH = pl.DeviceIdType.MESH


def encode(values):
    largest = jnp.maximum(jnp.max(jnp.abs(values), axis=0, keepdims=True), floor)
    level = jnp.ceil(jnp.log2(largest) * steps)
    inverse = top * jnp.exp2(level * (-1.0 / steps))
    codes = jnp.round(values * inverse).astype(jnp.int32).astype(jnp.int16)
    levels = jnp.broadcast_to(level, (pad, values.shape[1])).astype(jnp.int32).astype(jnp.int16)
    return codes, levels


def store_coded(ref, index, values):
    codes, levels = encode(values)
    size = values.shape[0]
    ref[index + (pl.ds(0, size),)] = codes
    ref[index + (pl.ds(size, pad),)] = levels


def load_coded(ref, index):
    size = ref.shape[-2] - pad
    level = ref[index + (pl.ds(size, pad),)].astype(jnp.int32).astype(jnp.float32)[:1]
    scale = jnp.exp2(level * (1.0 / steps)) * (1.0 / top)
    return ref[index + (pl.ds(0, size),)].astype(jnp.int32).astype(jnp.float32) * scale


def sweep_kernel(
    sizes, pos_ref, item_ref, uf_hbm, counts_hbm, items_hbm, ratings_hbm, x_ref, r_ref,
    vbuf, rbuf, start, pcur, part, sent, recv, tot, p_ref, res_ref, xacc, damp_ref, counts_ref,
    user_sem, count_sem, item_sem, rating_sem, v_send, v_recv, d_send, d_recv, t_send, t_recv,
    g_send, g_recv, in_send, in_recv, out_send,
):
    rows, cols, fibers = sizes
    half = cols // 2
    my_row, my_col, my_fiber = lax.axis_index("row"), lax.axis_index("col"), lax.axis_index("fiber")
    held_items = items_hbm.shape[0]
    share = held_items // fibers
    held_blocks, block = ratings_hbm.shape[0], ratings_hbm.shape[1]
    own_users = uf_hbm.shape[0] // block
    slots = cols * own_users
    per_user = pos_ref.shape[0] // slots
    chunk = held_blocks // CHUNKS

    left = 1 - lax.div(my_col, half)
    depth = left * my_col + (1 - left) * (cols - 1 - my_col)
    inner = my_col + 2 * left - 1
    outer = my_col - 2 * left + 1
    side = lax.div(depth + 1, half)

    def row_of(d):
        return lax.rem(my_row + d, rows)

    def col_of(d):
        return lax.rem(my_col + d, cols)

    def fiber_of(d):
        return lax.rem(my_fiber + d, fibers)

    item_load = pltpu.make_async_copy(items_hbm, vbuf.at[pl.ds(my_row * held_items, held_items)], item_sem)
    item_load.start()
    user_load = pltpu.make_async_copy(uf_hbm, x_ref, user_sem)
    user_load.start()
    count_load = pltpu.make_async_copy(counts_hbm, counts_ref, count_sem)
    count_load.start()

    def held_chunk(i):
        return pl.ds(my_fiber * held_blocks + i * chunk, chunk)

    rating_loads = []
    for i in range(CHUNKS):
        load = pltpu.make_async_copy(
            ratings_hbm.at[pl.ds(i * chunk, chunk)], rbuf.at[held_chunk(i)], rating_sem.at[i]
        )
        load.start()
        rating_loads.append(load)

    barrier = pltpu.get_barrier_semaphore()
    for d in range(1, rows):
        pl.semaphore_signal(barrier, inc=1, device_id={"row": row_of(d)}, device_id_type=MESH)
    for d in range(1, cols):
        pl.semaphore_signal(barrier, inc=1, device_id={"col": col_of(d)}, device_id_type=MESH)
    for d in range(1, fibers):
        pl.semaphore_signal(barrier, inc=1, device_id={"fiber": fiber_of(d)}, device_id_type=MESH)

    user_load.wait()
    for j in range(own_users):
        start[my_col * own_users + j] = x_ref[pl.ds(j * block, block), :].astype(jnp.bfloat16)
    item_load.wait()
    pl.semaphore_wait(barrier, rows + cols + fibers - 3)

    item_sends = []
    for d in range(1, rows):
        piece = pl.ds(my_row * held_items + my_fiber * share, share)
        copy = pltpu.make_async_remote_copy(
            src_ref=vbuf.at[piece],
            dst_ref=vbuf.at[piece],
            send_sem=v_send.at[d],
            recv_sem=v_recv.at[d],
            device_id={"row": row_of(d)},
            device_id_type=MESH,
        )
        copy.start()
        item_sends.append(copy)

    def start_copy(source, d, j):
        slot = source * own_users + j
        return pltpu.make_async_remote_copy(
            src_ref=start.at[slot],
            dst_ref=start.at[slot],
            send_sem=g_send.at[d, j],
            recv_sem=g_recv.at[slot],
            device_id={"col": col_of(d)},
            device_id_type=MESH,
        )

    for d in range(1, cols):
        for j in range(own_users):
            start_copy(my_col, d, j).start()
    rating_sends = []
    for i in range(CHUNKS):
        rating_loads[i].wait()
        for e in range(1, fibers):
            copy = pltpu.make_async_remote_copy(
                src_ref=rbuf.at[held_chunk(i)],
                dst_ref=rbuf.at[held_chunk(i)],
                send_sem=t_send.at[e, i],
                recv_sem=t_recv.at[e, i],
                device_id={"fiber": fiber_of(e)},
                device_id_type=MESH,
            )
            copy.start()
            rating_sends.append(copy)

    count_load.wait()
    damp_ref[...] = jnp.zeros_like(damp_ref)
    xacc[...] = jnp.zeros_like(xacc)
    for j in range(own_users):
        scaled = reg_weight * counts_ref[pl.ds(j, 1), :].astype(jnp.float32)
        across = jnp.broadcast_to(scaled, (block, block))
        own = my_col * own_users + j
        damp_ref[own] = jnp.broadcast_to(jnp.transpose(across)[:, :1], (block, damp_ref.shape[2]))
        xacc[own] = x_ref[pl.ds(j * block, block), :]

    shared = []
    for d in range(1, rows):
        item_sends[d - 1].wait_recv()
        source = lax.rem(my_row + rows - d, rows)
        piece = pl.ds(source * held_items + my_fiber * share, share)
        for e in range(1, fibers):
            copy = pltpu.make_async_remote_copy(
                src_ref=vbuf.at[piece],
                dst_ref=vbuf.at[piece],
                send_sem=d_send.at[d, e],
                recv_sem=d_recv.at[d, e],
                device_id={"fiber": fiber_of(e)},
                device_id_type=MESH,
            )
            copy.start()
            shared.append(copy)
    for copy in rating_sends + shared:
        copy.wait_recv()

    def inward(stage, u):
        return pltpu.make_async_remote_copy(
            src_ref=sent.at[stage, u],
            dst_ref=recv.at[side, stage, u],
            send_sem=in_send.at[stage, u],
            recv_sem=in_recv.at[side, stage, u],
            device_id={"col": inner},
            device_id_type=MESH,
        )

    def outward(stage, u):
        return pltpu.make_async_remote_copy(
            src_ref=tot.at[stage, u],
            dst_ref=recv.at[1, stage, u],
            send_sem=out_send.at[stage, u],
            recv_sem=in_recv.at[1, stage, u],
            device_id={"col": outer},
            device_id_type=MESH,
        )

    def arrival(which, stage, u):
        return pltpu.make_async_remote_copy(
            src_ref=sent.at[stage, u],
            dst_ref=recv.at[which, stage, u],
            send_sem=in_send.at[stage, u],
            recv_sem=in_recv.at[which, stage, u],
            device_id={"col": inner},
            device_id_type=MESH,
        )

    def terms(stage, u):
        rows_of_user = start[u] if stage == 0 else pcur[u]
        base = u * per_user
        items = jnp.concatenate([vbuf[item_ref[base + i]] for i in range(per_user)], axis=0)
        ratings = jnp.concatenate([rbuf[pos_ref[base + i]] for i in range(per_user)], axis=1)
        predicted = lax.dot_general(
            rows_of_user, items, (((1,), (1,)), ((), ())), preferred_element_type=jnp.float32
        )
        ratings = ratings.astype(jnp.float32)
        if stage == 0:
            weights = jnp.where(ratings != 0, ratings - predicted, 0.0)
        else:
            weights = jnp.where(ratings != 0, predicted, 0.0)
        total = jnp.dot(weights.astype(jnp.bfloat16), items, preferred_element_type=jnp.float32)
        if stage == 0:
            return total - damp_ref[u] * xacc[u]
        return total + damp_ref[u] * p_ref[u]

    def compute(stage, u):
        part[u] = terms(stage, u)

        @pl.when(depth == 0)
        def _():
            store_coded(sent, (stage, u), part[u])
            inward(stage, u).start()

    def pass_on(stage, u):
        @pl.when(depth > 0)
        def _():
            arrival(0, stage, u).wait_recv()
            store_coded(sent, (stage, u), part[u] + load_coded(recv, (0, stage, u)))
            inward(stage, u).start()

    def collect(stage, u):
        arrival(1, stage, u).wait_recv()

        @pl.when(depth == half - 1)
        def _():
            store_coded(tot, (stage, u), load_coded(sent, (stage, u)) + load_coded(recv, (1, stage, u)))

        @pl.when(depth < half - 1)
        def _():
            tot[stage, u] = recv[1, stage, u]

        @pl.when(depth > 0)
        def _():
            outward(stage, u).start()

    def update(stage, u):
        image = load_coded(tot, (stage, u))
        if stage == 0:
            res_ref[u] = image
            p_ref[u] = image
            pcur[u] = image.astype(jnp.bfloat16)
            return
        direction = p_ref[u]
        residual = res_ref[u]
        square = jnp.sum(residual * residual, axis=1, keepdims=True)
        step_size = square / (jnp.sum(direction * image, axis=1, keepdims=True) + tiny)
        residual = residual - step_size * image
        res_ref[u] = residual
        xacc[u] = xacc[u] + step_size * direction
        if stage < ITERS:
            renewed = jnp.sum(residual * residual, axis=1, keepdims=True)
            direction = residual + renewed / (square + tiny) * direction
            p_ref[u] = direction
            pcur[u] = direction.astype(jnp.bfloat16)

    order = sorted(range(cols), key=lambda c: (abs(2 * c - cols + 1), c))
    order = [c * own_users + j for c in order for j in range(own_users)]
    for u in order:
        @pl.when(my_col != u // own_users)
        def _():
            start_copy(u // own_users, 1, u % own_users).wait_recv()

        compute(0, u)
    for u in order:
        pass_on(0, u)
    for stage in range(ITERS):
        for u in order:
            collect(stage, u)
            update(stage, u)
            compute(stage + 1, u)
        for u in order:
            pass_on(stage + 1, u)
    for u in order:
        collect(ITERS, u)
    for j in range(own_users):
        own = my_col * own_users + j
        update(ITERS, own)
        users = pl.ds(j * block, block)
        x_ref[users, :] = xacc[own]
        r_ref[users, :] = res_ref[own]

    for copy in item_sends + rating_sends + shared:
        copy.wait_send()
    for d in range(1, cols):
        for j in range(own_users):
            start_copy(my_col, d, j).wait_send()
    for stage in range(ITERS + 1):
        for u in order:
            inward(stage, u).wait_send()

    @pl.when(depth > 0)
    def _():
        for stage in range(ITERS + 1):
            for u in order:
                outward(stage, u).wait_send()


def per_device(sizes, slab_users, user_factors, item_factors, ratings, block_user, block_item, counts):
    rows, cols, fibers = sizes
    held_blocks, block = ratings.shape[2], ratings.shape[3]
    rank = user_factors.shape[1]
    users = user_factors.shape[0]
    own_users = users // block
    item_blocks = item_factors.shape[0] // block
    per_user = fibers * held_blocks // (slab_users // block)

    both = lax.all_gather(jnp.stack([block_user[0, 0], block_item[0, 0]]), "fiber", axis=0)
    owners = both[:, 0].reshape(-1)
    columns = both[:, 1].reshape(-1)
    here = jnp.arange(owners.shape[0], dtype=jnp.int32)
    keys = owners * owners.shape[0] + here
    ranks = jnp.sum((keys[None, :] < keys[:, None]).astype(jnp.int32), axis=1)
    groups = jnp.arange(cols, dtype=jnp.int32)[:, None] * fibers + lax.axis_index("fiber")
    wanted = (
        groups[:, :, None] * (own_users * per_user)
        + jnp.arange(own_users * per_user, dtype=jnp.int32)[None, None, :]
    ).reshape(-1)
    match = wanted[:, None] == ranks[None, :]
    positions = jnp.sum(jnp.where(match, here[None, :], 0), axis=1)
    items = jnp.sum(jnp.where(match, columns[None, :], 0), axis=1)

    stages = ITERS + 1
    slots = cols * own_users
    dma = pltpu.SemaphoreType.DMA
    vmem = pl.BlockSpec(memory_space=pltpu.VMEM)
    smem = pl.BlockSpec(memory_space=pltpu.SMEM)
    hbm = pl.BlockSpec(memory_space=pl.ANY)
    return pl.pallas_call(
        functools.partial(sweep_kernel, sizes),
        out_shape=(
            jax.ShapeDtypeStruct((users, rank), jnp.float32),
            jax.ShapeDtypeStruct((users, rank), jnp.float32),
        ),
        in_specs=[smem, smem, hbm, hbm, hbm, hbm],
        out_specs=(vmem, vmem),
        scratch_shapes=[
            pltpu.VMEM((rows * item_blocks, block, rank), jnp.bfloat16),
            pltpu.VMEM((fibers * held_blocks, block, block), jnp.bfloat16),
            pltpu.VMEM((slots, block, rank), jnp.bfloat16),
            pltpu.VMEM((slots, block, rank), jnp.bfloat16),
            pltpu.VMEM((slots, block, rank), jnp.float32),
            pltpu.VMEM((stages, slots, block + pad, rank), jnp.int16),
            pltpu.VMEM((2, stages, slots, block + pad, rank), jnp.int16),
            pltpu.VMEM((stages, slots, block + pad, rank), jnp.int16),
            pltpu.VMEM((slots, block, rank), jnp.float32),
            pltpu.VMEM((slots, block, rank), jnp.float32),
            pltpu.VMEM((slots, block, rank), jnp.float32),
            pltpu.VMEM((slots, block, rank), jnp.float32),
            pltpu.VMEM((own_users, block), jnp.int32),
            dma,
            dma,
            dma,
            dma((CHUNKS,)),
            dma((rows,)),
            dma((rows,)),
            dma((rows, fibers)),
            dma((rows, fibers)),
            dma((fibers, CHUNKS)),
            dma((fibers, CHUNKS)),
            dma((cols, own_users)),
            dma((slots,)),
            dma((stages, slots)),
            dma((2, stages, slots)),
            dma((stages, slots)),
        ],
        compiler_params=pltpu.CompilerParams(
            collective_id=0, has_side_effects=True, vmem_limit_bytes=67043328
        ),
    )(
        positions,
        items,
        user_factors,
        counts.reshape(own_users, block),
        item_factors.reshape(item_blocks, block, rank),
        ratings[0, 0],
    )


def solution(mesh):
    sizes = (mesh.shape["row"], mesh.shape["col"], mesh.shape["fiber"])

    def whole(user_factors, item_factors, ratings, block_user, block_item, counts):
        slab_users = user_factors.shape[0] // sizes[0]
        return jax.shard_map(
            functools.partial(per_device, sizes, slab_users),
            mesh=mesh,
            in_specs=(
                P(("row", "col", "fiber"), None),
                P(("row", "col"), None),
                P("row", "col", "fiber", None, None),
                P("row", "col", "fiber"),
                P("row", "col", "fiber"),
                P(("row", "col", "fiber")),
            ),
            out_specs=(P(("row", "col", "fiber"), None), P(("row", "col", "fiber"), None)),
            check_vma=False,
        )(user_factors, item_factors, ratings, block_user, block_item, counts)

    return whole
```

time: 68 us -> 64.3 us (0.946)
  Pallas kernels: 60.3 us -> 56.6 us
    pallas_call x1, Pallas kernels: 60.3 us -> 56.6 us  [per_device(): pl.pallas_call(functools.partial(sweep_kernel, sizes), out_shape=(jax.Sha...]
where the time goes in v1:
time: 64.3 us; the launch traced here: 64.1 us
  Pallas kernels  56.6 us (88%)
  local copies, waits for them, and re-layouts  3.22 us (5%)
  blocking collectives  1.95 us (3%)
  other arithmetic  1.66 us (3%)
  between operations  0.65 us (1%)
    pallas_call x1, Pallas kernels, per_device(): pl.pallas_call(functools.partial(sweep_kernel, sizes), out_shape=(jax.Sha...  56.6 us
    unnamed x2, local copies, waits for them, and re-layouts  3.14 us
    all_gather x1, blocking collectives, per_device(): lax.all_gather(jnp.stack([block_user[0, 0], block_item[0, 0]]), 'fiber',...  1.95 us

profile of v1, /device:TPU:0, one launch (start us, length us, event | category | flops | bytes accessed | tf_op | source)
XLA Modules:
  0.0 64.1 jit_solution(139340252987939337)
XLA Ops:
  0.6 0.7 %add_bitcast_fusion = s32[1,2,128]{2,1,0:T(2,128)S(1)} fusion(s32[1,128]{1,0:T(1,128)} %bitcast.16, s32[1,128]{1,0:T(1,128)} %bitcast.17), kind=kLoop, calls=%fused_computation.7 | loop fusion | flops 256 | bytes 2048
  1.3 1.9 %all-gather.1 = s32[2,2,128]{2,1,0:T(2,128)S(1)} all-gather(s32[1,2,128]{2,1,0:T(2,128)S(1)} %add_bitcast_fusion), channel_id=2, replica_groups=mesh['row'=4,'col'=4,'fiber'=2] {'fiber'}, dimensions={0}, use_global_device_ids=true | all-gather | bytes 3072 | tf_op jit(solution)/shard_map/all_gather | solution.py:332
  3.3 0.2 convert_reduce_fusion
  3.5 0.1 iota_add_fusion
  3.5 0.1 add.51
  3.6 0.7 %fusion.1 = (s32[128]{0:T(128)}, s32[128]{0:T(128)}) fusion(s32[256]{0:T(256)S(1)} %bitcast.13, s32[256]{0:T(256)S(1)} %convert_reduce_fusion, s32[128]{0:T(128)S(1)} %add.51), kind=kLoop, calls=%fused_computation.4 | loop fusion | flops 163584 | bytes 3584 | tf_op jit(solution)/shard_map/reduce_sum | solution.py:345
  4.3 56.6 %shard_map.77 = (f32[256,128]{1,0:T(8,128)}, f32[256,128]{1,0:T(8,128)}) custom-call(s32[128]{0:T(128)} %get-tuple-element.3.pos_ref, s32[128]{0:T(128)} %get-tuple-element.2.item_ref, f32[256,128]{1,0:T(8,128)} %uf_hbm.1, s32[2,128]{1,0:T(2,128)} %bitcast.15, bf16[8,128,128]{2,1,0:T(8,128)(2,1)} %bitcast.12, bf16[128,128,128]{2,1,0:T(8,128)(2,1)} %bitcast.11), custom_call_target="tpu_custom_call" | custom-call | tf_op jit(solution)/shard_map/pallas_call | solution.py:353
  61.0 1.6 %copy.10 = f32[256,128]{1,0:T(8,128)} copy(f32[256,128]{1,0:T(8,128)} %get-tuple-element.8) | data formatting | bytes 262144
  62.5 1.6 %copy.11 = f32[256,128]{1,0:T(8,128)} copy(f32[256,128]{1,0:T(8,128)} %get-tuple-element.9) | data formatting | bytes 262144
  (3 shorter events, 0.0 us)

commit v2 on v1

--- a/solution.py
+++ b/solution.py
@@ -9,6 +9,7 @@
 
 ITERS = 2
 CHUNKS = 4
+LAG = 3
 
 reg_weight = 0.0004
 tiny = 1e-06
@@ -45,20 +46,23 @@
 
 
 def sweep_kernel(
-    sizes, pos_ref, item_ref, uf_hbm, counts_hbm, items_hbm, ratings_hbm, x_ref, r_ref,
-    vbuf, rbuf, start, pcur, part, sent, recv, tot, p_ref, res_ref, xacc, damp_ref, counts_ref,
-    user_sem, count_sem, item_sem, rating_sem, v_send, v_recv, d_send, d_recv, t_send, t_recv,
-    g_send, g_recv, in_send, in_recv, out_send,
+    sizes, owner_hbm, column_hbm, uf_hbm, counts_hbm, items_hbm, ratings_hbm, x_ref, r_ref,
+    vbuf, rbuf, start, pcur, part, sent, recv, tot, last, p_ref, res_ref, xacc, damp_ref, counts_ref,
+    ids, places, pos_ref, user_sem, count_sem, id_sem, place_sem, item_sem, rating_sem, i_send, i_recv,
+    v_send, v_recv, d_send, d_recv, t_send, t_recv,
+    g_send, g_recv, in_send, in_recv, out_send, f_send, f_recv,
 ):
     rows, cols, fibers = sizes
     half = cols // 2
     my_row, my_col, my_fiber = lax.axis_index("row"), lax.axis_index("col"), lax.axis_index("fiber")
     held_items = items_hbm.shape[0]
     share = held_items // fibers
+    parts = 2 if rows == 4 and share % 2 == 0 else 1
+    piece = share // parts
     held_blocks, block = ratings_hbm.shape[0], ratings_hbm.shape[1]
     own_users = uf_hbm.shape[0] // block
     slots = cols * own_users
-    per_user = pos_ref.shape[0] // slots
+    per_user = pos_ref.shape[1] // slots
     chunk = held_blocks // CHUNKS
 
     left = 1 - lax.div(my_col, half)
@@ -76,6 +80,12 @@
     def fiber_of(d):
         return lax.rem(my_fiber + d, fibers)
 
+    id_loads = [
+        pltpu.make_async_copy(source, ids.at[my_fiber, i], id_sem.at[i])
+        for i, source in enumerate((owner_hbm, column_hbm))
+    ]
+    for load in id_loads:
+        load.start()
     item_load = pltpu.make_async_copy(items_hbm, vbuf.at[pl.ds(my_row * held_items, held_items)], item_sem)
     item_load.start()
     user_load = pltpu.make_async_copy(uf_hbm, x_ref, user_sem)
@@ -105,22 +115,57 @@
     user_load.wait()
     for j in range(own_users):
         start[my_col * own_users + j] = x_ref[pl.ds(j * block, block), :].astype(jnp.bfloat16)
+    for load in id_loads:
+        load.wait()
     item_load.wait()
     pl.semaphore_wait(barrier, rows + cols + fibers - 3)
 
-    item_sends = []
-    for d in range(1, rows):
-        piece = pl.ds(my_row * held_items + my_fiber * share, share)
+    id_sends = []
+    for e in range(1, fibers):
         copy = pltpu.make_async_remote_copy(
-            src_ref=vbuf.at[piece],
-            dst_ref=vbuf.at[piece],
-            send_sem=v_send.at[d],
-            recv_sem=v_recv.at[d],
-            device_id={"row": row_of(d)},
+            src_ref=ids.at[my_fiber],
+            dst_ref=ids.at[my_fiber],
+            send_sem=i_send.at[e],
+            recv_sem=i_recv.at[e],
+            device_id={"fiber": fiber_of(e)},
             device_id_type=MESH,
         )
         copy.start()
-        item_sends.append(copy)
+        id_sends.append(copy)
+
+    def item_piece(row, i):
+        return pl.ds(row * held_items + my_fiber * share + i * piece, piece)
+
+    def item_copy(source, d, i, target):
+        return pltpu.make_async_remote_copy(
+            src_ref=vbuf.at[item_piece(source, i)],
+            dst_ref=vbuf.at[item_piece(source, i)],
+            send_sem=v_send.at[d, i],
+            recv_sem=v_recv.at[d, i],
+            device_id={"row": target},
+            device_id_type=MESH,
+        )
+
+    if parts == 2:
+        across = my_row + 1 - 2 * lax.rem(my_row, 2)
+        along = my_row + 2 - 4 * lax.div(my_row, 2)
+        corner = 3 - my_row
+        peers = [my_row, across, along, corner]
+        first = [item_copy(my_row, 1, 0, across), item_copy(my_row, 2, 1, along)]
+        first += [item_copy(my_row, 1, 1, across), item_copy(my_row, 2, 0, along)]
+        relays = [
+            (item_copy(across, 1, 0, across), item_copy(across, 3, 0, along)),
+            (item_copy(along, 2, 1, along), item_copy(along, 3, 1, across)),
+        ]
+        landed = [(1, 1), (2, 0), (3, 0), (3, 1)]
+    else:
+        peers = [lax.rem(my_row + rows - d, rows) for d in range(rows)]
+        first = [item_copy(my_row, d, 0, row_of(d)) for d in range(1, rows)]
+        relays = []
+        landed = [(d, 0) for d in range(1, rows)]
+    for copy in first:
+        copy.start()
+    item_sends = first + [onward for _, onward in relays]
 
     def start_copy(source, d, j):
         slot = source * own_users + j
@@ -161,22 +206,56 @@
         damp_ref[own] = jnp.broadcast_to(jnp.transpose(across)[:, :1], (block, damp_ref.shape[2]))
         xacc[own] = x_ref[pl.ds(j * block, block), :]
 
+    for copy in id_sends:
+        copy.wait_recv()
+    total_blocks = fibers * held_blocks
+    lanes = (held_blocks, held_blocks)
+    here = lax.broadcasted_iota(jnp.int32, lanes, 0)
+    lane = lax.broadcasted_iota(jnp.int32, lanes, 1)
+    group = own_users * per_user
+    ahead = sum(jnp.where(lane >= c * group, 1, 0) for c in range(1, cols))
+    wanted = lane + (ahead * (fibers - 1) + my_fiber) * group
+    keys = [jnp.broadcast_to(ids[e, 0], lanes) * total_blocks + lane + e * held_blocks for e in range(fibers)]
+    standing = [jnp.transpose(key) for key in keys]
+    found_place = jnp.zeros((1, held_blocks), jnp.int32)
+    found_item = jnp.zeros((1, held_blocks), jnp.int32)
+    for e in range(fibers):
+        before = sum(jnp.where(other < keys[e], 1, 0) for other in standing)
+        rank = jnp.sum(before, axis=0, keepdims=True)
+        match = jnp.transpose(jnp.broadcast_to(rank, lanes)) == wanted
+        column = jnp.transpose(jnp.broadcast_to(ids[e, 1], lanes))
+        found_place += jnp.sum(jnp.where(match, here + e * held_blocks, 0), axis=0, keepdims=True)
+        found_item += jnp.sum(jnp.where(match, column, 0), axis=0, keepdims=True)
+    places[0:1, :] = found_place
+    places[1:2, :] = found_item
+    place_copy = pltpu.make_async_copy(places, pos_ref, place_sem)
+    place_copy.start()
+
     shared = []
-    for d in range(1, rows):
-        item_sends[d - 1].wait_recv()
-        source = lax.rem(my_row + rows - d, rows)
-        piece = pl.ds(source * held_items + my_fiber * share, share)
+
+    def share_piece(d, i):
         for e in range(1, fibers):
             copy = pltpu.make_async_remote_copy(
-                src_ref=vbuf.at[piece],
-                dst_ref=vbuf.at[piece],
-                send_sem=d_send.at[d, e],
-                recv_sem=d_recv.at[d, e],
+                src_ref=vbuf.at[item_piece(peers[d], i)],
+                dst_ref=vbuf.at[item_piece(peers[d], i)],
+                send_sem=d_send.at[d, i, e],
+                recv_sem=d_recv.at[d, i, e],
                 device_id={"fiber": fiber_of(e)},
                 device_id_type=MESH,
             )
             copy.start()
             shared.append(copy)
+
+    for arrived, onward in relays:
+        arrived.wait_recv()
+        onward.start()
+    if parts == 2:
+        share_piece(1, 0)
+        share_piece(2, 1)
+    for d, i in landed:
+        item_copy(peers[d], d, i, my_row).wait_recv()
+        share_piece(d, i)
+    place_copy.wait()
     for copy in rating_sends + shared:
         copy.wait_recv()
 
@@ -213,8 +292,8 @@
     def terms(stage, u):
         rows_of_user = start[u] if stage == 0 else pcur[u]
         base = u * per_user
-        items = jnp.concatenate([vbuf[item_ref[base + i]] for i in range(per_user)], axis=0)
-        ratings = jnp.concatenate([rbuf[pos_ref[base + i]] for i in range(per_user)], axis=1)
+        items = jnp.concatenate([vbuf[pos_ref[1, base + i]] for i in range(per_user)], axis=0)
+        ratings = jnp.concatenate([rbuf[pos_ref[0, base + i]] for i in range(per_user)], axis=1)
         predicted = lax.dot_general(
             rows_of_user, items, (((1,), (1,)), ((), ())), preferred_element_type=jnp.float32
         )
@@ -228,8 +307,25 @@
             return total - damp_ref[u] * xacc[u]
         return total + damp_ref[u] * p_ref[u]
 
+    def deliver(d, j, target, source):
+        return pltpu.make_async_remote_copy(
+            src_ref=sent.at[ITERS, target * own_users + j],
+            dst_ref=last.at[source, j],
+            send_sem=f_send.at[d, j],
+            recv_sem=f_recv.at[source, j],
+            device_id={"col": target},
+            device_id_type=MESH,
+        )
+
     def compute(stage, u):
         part[u] = terms(stage, u)
+        if stage == ITERS:
+            @pl.when(my_col != u // own_users)
+            def _():
+                store_coded(sent, (stage, u), part[u])
+                deliver(u // own_users, u % own_users, u // own_users, my_col).start()
+
+            return
 
         @pl.when(depth == 0)
         def _():
@@ -258,8 +354,9 @@
         def _():
             outward(stage, u).start()
 
-    def update(stage, u):
-        image = load_coded(tot, (stage, u))
+    def update(stage, u, image=None):
+        if stage < ITERS:
+            image = load_coded(tot, (stage, u))
         if stage == 0:
             res_ref[u] = image
             p_ref[u] = image
@@ -286,77 +383,64 @@
             start_copy(u // own_users, 1, u % own_users).wait_recv()
 
         compute(0, u)
-    for u in order:
-        pass_on(0, u)
     for stage in range(ITERS):
-        for u in order:
-            collect(stage, u)
-            update(stage, u)
-            compute(stage + 1, u)
-        for u in order:
-            pass_on(stage + 1, u)
-    for u in order:
-        collect(ITERS, u)
+        for step in range(slots + LAG):
+            if step < slots:
+                pass_on(stage, order[step])
+            if step >= LAG:
+                u = order[step - LAG]
+                collect(stage, u)
+                update(stage, u)
+                compute(stage + 1, u)
     for j in range(own_users):
         own = my_col * own_users + j
-        update(ITERS, own)
+        image = part[own]
+        for d in range(1, cols):
+            source = col_of(d)
+            deliver(d, j, my_col, source).wait_recv()
+            image = image + load_coded(last, (source, j))
+        update(ITERS, own, image)
         users = pl.ds(j * block, block)
         x_ref[users, :] = xacc[own]
         r_ref[users, :] = res_ref[own]
 
-    for copy in item_sends + rating_sends + shared:
+    for copy in item_sends + rating_sends + shared + id_sends:
         copy.wait_send()
     for d in range(1, cols):
         for j in range(own_users):
             start_copy(my_col, d, j).wait_send()
-    for stage in range(ITERS + 1):
+            deliver(col_of(d), j, col_of(d), my_col).wait_send()
+    for stage in range(ITERS):
         for u in order:
             inward(stage, u).wait_send()
 
     @pl.when(depth > 0)
     def _():
-        for stage in range(ITERS + 1):
+        for stage in range(ITERS):
             for u in order:
                 outward(stage, u).wait_send()
 
 
-def per_device(sizes, slab_users, user_factors, item_factors, ratings, block_user, block_item, counts):
+def per_device(sizes, user_factors, item_factors, ratings, block_user, block_item, counts):
     rows, cols, fibers = sizes
     held_blocks, block = ratings.shape[2], ratings.shape[3]
     rank = user_factors.shape[1]
     users = user_factors.shape[0]
     own_users = users // block
     item_blocks = item_factors.shape[0] // block
-    per_user = fibers * held_blocks // (slab_users // block)
-
-    both = lax.all_gather(jnp.stack([block_user[0, 0], block_item[0, 0]]), "fiber", axis=0)
-    owners = both[:, 0].reshape(-1)
-    columns = both[:, 1].reshape(-1)
-    here = jnp.arange(owners.shape[0], dtype=jnp.int32)
-    keys = owners * owners.shape[0] + here
-    ranks = jnp.sum((keys[None, :] < keys[:, None]).astype(jnp.int32), axis=1)
-    groups = jnp.arange(cols, dtype=jnp.int32)[:, None] * fibers + lax.axis_index("fiber")
-    wanted = (
-        groups[:, :, None] * (own_users * per_user)
-        + jnp.arange(own_users * per_user, dtype=jnp.int32)[None, None, :]
-    ).reshape(-1)
-    match = wanted[:, None] == ranks[None, :]
-    positions = jnp.sum(jnp.where(match, here[None, :], 0), axis=1)
-    items = jnp.sum(jnp.where(match, columns[None, :], 0), axis=1)
 
     stages = ITERS + 1
     slots = cols * own_users
     dma = pltpu.SemaphoreType.DMA
     vmem = pl.BlockSpec(memory_space=pltpu.VMEM)
-    smem = pl.BlockSpec(memory_space=pltpu.SMEM)
     hbm = pl.BlockSpec(memory_space=pl.ANY)
-    return pl.pallas_call(
+    return hand_out(*pl.pallas_call(
         functools.partial(sweep_kernel, sizes),
         out_shape=(
             jax.ShapeDtypeStruct((users, rank), jnp.float32),
             jax.ShapeDtypeStruct((users, rank), jnp.float32),
         ),
-        in_specs=[smem, smem, hbm, hbm, hbm, hbm],
+        in_specs=[hbm] * 6,
         out_specs=(vmem, vmem),
         scratch_shapes=[
             pltpu.VMEM((rows * item_blocks, block, rank), jnp.bfloat16),
@@ -365,49 +449,79 @@
             pltpu.VMEM((slots, block, rank), jnp.bfloat16),
             pltpu.VMEM((slots, block, rank), jnp.float32),
             pltpu.VMEM((stages, slots, block + pad, rank), jnp.int16),
-            pltpu.VMEM((2, stages, slots, block + pad, rank), jnp.int16),
-            pltpu.VMEM((stages, slots, block + pad, rank), jnp.int16),
+            pltpu.VMEM((2, ITERS, slots, block + pad, rank), jnp.int16),
+            pltpu.VMEM((ITERS, slots, block + pad, rank), jnp.int16),
+            pltpu.VMEM((cols, own_users, block + pad, rank), jnp.int16),
             pltpu.VMEM((slots, block, rank), jnp.float32),
             pltpu.VMEM((slots, block, rank), jnp.float32),
             pltpu.VMEM((slots, block, rank), jnp.float32),
             pltpu.VMEM((slots, block, rank), jnp.float32),
             pltpu.VMEM((own_users, block), jnp.int32),
+            pltpu.VMEM((fibers, 2, 1, held_blocks), jnp.int32),
+            pltpu.VMEM((2, held_blocks), jnp.int32),
+            pltpu.SMEM((2, held_blocks), jnp.int32),
             dma,
+            dma,
+            dma((2,)),
             dma,
             dma,
             dma((CHUNKS,)),
-            dma((rows,)),
-            dma((rows,)),
-            dma((rows, fibers)),
-            dma((rows, fibers)),
+            dma((fibers,)),
+            dma((fibers,)),
+            dma((rows, 2)),
+            dma((rows, 2)),
+            dma((rows, 2, fibers)),
+            dma((rows, 2, fibers)),
             dma((fibers, CHUNKS)),
             dma((fibers, CHUNKS)),
             dma((cols, own_users)),
             dma((slots,)),
-            dma((stages, slots)),
-            dma((2, stages, slots)),
-            dma((stages, slots)),
+            dma((ITERS, slots)),
+            dma((2, ITERS, slots)),
+            dma((ITERS, slots)),
+            dma((cols, own_users)),
+            dma((cols, own_users)),
         ],
         compiler_params=pltpu.CompilerParams(
             collective_id=0, has_side_effects=True, vmem_limit_bytes=67043328
         ),
     )(
-        positions,
-        items,
+        block_user[0],
+        block_item[0],
         user_factors,
         counts.reshape(own_users, block),
         item_factors.reshape(item_blocks, block, rank),
         ratings[0, 0],
-    )
+    ))
+
+
+def tail_kernel(x_ref, r_ref, xo_ref, ro_ref, sems):
+    a = pltpu.make_async_copy(x_ref, xo_ref, sems.at[0])
+    b = pltpu.make_async_copy(r_ref, ro_ref, sems.at[1])
+    a.start()
+    b.start()
+    a.wait()
+    b.wait()
+
+
+def hand_out(x, r):
+    vmem = pl.BlockSpec(memory_space=pltpu.VMEM)
+    hbm = pl.BlockSpec(memory_space=pl.ANY)
+    return pl.pallas_call(
+        tail_kernel,
+        out_shape=(jax.ShapeDtypeStruct(x.shape, x.dtype), jax.ShapeDtypeStruct(r.shape, r.dtype)),
+        in_specs=[vmem, vmem],
+        out_specs=(hbm, hbm),
+        scratch_shapes=[pltpu.SemaphoreType.DMA((2,))],
+    )(x, r)
 
 
 def solution(mesh):
     sizes = (mesh.shape["row"], mesh.shape["col"], mesh.shape["fiber"])
 
     def whole(user_factors, item_factors, ratings, block_user, block_item, counts):
-        slab_users = user_factors.shape[0] // sizes[0]
         return jax.shard_map(
-            functools.partial(per_device, sizes, slab_users),
+            functools.partial(per_device, sizes),
             mesh=mesh,
             in_specs=(
                 P(("row", "col", "fiber"), None),

time: 64.3 us -> 50.9 us (0.79)
  Pallas kernels: 56.6 us -> 50.1 us
  local copies, waits for them, and re-layouts: 3.22 us -> 0 us
  blocking collectives: 1.95 us -> 0 us
  other arithmetic: 1.66 us -> 0 us
    pallas_call x1, Pallas kernels: 56.6 us -> 48.4 us  [per_device(): pl.pallas_call(functools.partial(sweep_kernel, sizes), out_shape=(jax.Sha...]
    unnamed x2 -> x0, local copies, waits for them, and re-layouts: 3.14 us -> none
    all_gather x1 -> x0, blocking collectives: 1.95 us -> none  [per_device(): lax.all_gather(jnp.stack([block_user[0, 0], block_item[0, 0]]), 'fiber',...]
    pallas_call x0 -> x1, Pallas kernels: none -> 1.68 us  [hand_out(): pl.pallas_call(tail_kernel, out_shape=(jax.ShapeDtypeStruct(x.shape, x.dt...]
    reduce_sum x2 -> x0, other arithmetic: 0.89 us -> none  [the longest x1 0.71 us: per_device(): items = jnp.sum(jnp.where(match, columns[None, :], 0), axis=1)]
    unnamed x1 -> x0, other arithmetic: 0.68 us -> none
where the time goes in v2:
time: 50.9 us; the launch traced here: 50.7 us
  Pallas kernels  50.1 us (98%)
  between operations  0.64 us (1%)
    pallas_call x1, Pallas kernels, per_device(): pl.pallas_call(functools.partial(sweep_kernel, sizes), out_shape=(jax.Sha...  48.4 us
    pallas_call x1, Pallas kernels, hand_out(): pl.pallas_call(tail_kernel, out_shape=(jax.ShapeDtypeStruct(x.shape, x.dt...  1.68 us

profile of v2, /device:TPU:0, one launch (start us, length us, event | category | flops | bytes accessed | tf_op | source)
XLA Modules:
  0.0 50.7 jit_solution(4556024114266519943)
XLA Ops:
  0.6 48.4 %shard_map.77 = (f32[256,128]{1,0:T(8,128)}, f32[256,128]{1,0:T(8,128)}) custom-call(s32[1,128]{1,0:T(1,128)} %bitcast.8, s32[1,128]{1,0:T(1,128)} %bitcast.9, f32[256,128]{1,0:T(8,128)} %uf_hbm.1, s32[2,128]{1,0:T(2,128)} %bitcast.7, bf16[8,128,128]{2,1,0:T(8,128)(2,1)} %bitcast.6, bf16[128,128,128]{2,1,0:T(8,128)(2,1)} %bitcast.5), custom_call_target="tpu_custom_call" | custom-call | tf_op jit(solution)/shard_map/pallas_call | solution.py:437
  49.0 1.7 %shard_map.78 = (f32[256,128]{1,0:T(8,128)}, f32[256,128]{1,0:T(8,128)}) custom-call(f32[256,128]{1,0:T(8,128)} %get-tuple-element.4.x_ref, f32[256,128]{1,0:T(8,128)} %get-tuple-element.5.r_ref), custom_call_target="tpu_custom_call" | custom-call | tf_op jit(solution)/shard_map/pallas_call | solution.py:510

commit v3 on v2

--- a/solution.py
+++ b/solution.py
@@ -17,7 +17,7 @@
 top = 32700.0
 steps = 128.0
 floor = 2.0**-100
-pad = 16
+pad = 8
 
 MESH = pl.DeviceIdType.MESH
 
@@ -375,7 +375,7 @@
             p_ref[u] = direction
             pcur[u] = direction.astype(jnp.bfloat16)
 
-    order = sorted(range(cols), key=lambda c: (abs(2 * c - cols + 1), c))
+    order = sorted(range(cols), key=lambda c: (-abs(2 * c - cols + 1), c))
     order = [c * own_users + j for c in order for j in range(own_users)]
     for u in order:
         @pl.when(my_col != u // own_users)

time: 50.9 us -> 49.5 us (0.972)
  Pallas kernels: 50.1 us -> 48.7 us
    pallas_call x1, Pallas kernels: 48.4 us -> 47 us  [per_device(): pl.pallas_call(functools.partial(sweep_kernel, sizes), out_shape=(jax.Sha...]
where the time goes in v3:
time: 49.5 us; the launch traced here: 49.3 us
  Pallas kernels  48.7 us (98%)
  between operations  0.64 us (1%)
    pallas_call x1, Pallas kernels, per_device(): pl.pallas_call(functools.partial(sweep_kernel, sizes), out_shape=(jax.Sha...  47 us
    pallas_call x1, Pallas kernels, hand_out(): pl.pallas_call(tail_kernel, out_shape=(jax.ShapeDtypeStruct(x.shape, x.dt...  1.68 us

profile of v3, /device:TPU:0, one launch (start us, length us, event | category | flops | bytes accessed | tf_op | source)
XLA Modules:
  0.0 49.3 jit_solution(2842264839189480096)
XLA Ops:
  0.6 47.0 %shard_map.77 = (f32[256,128]{1,0:T(8,128)}, f32[256,128]{1,0:T(8,128)}) custom-call(s32[1,128]{1,0:T(1,128)} %bitcast.8, s32[1,128]{1,0:T(1,128)} %bitcast.9, f32[256,128]{1,0:T(8,128)} %uf_hbm.1, s32[2,128]{1,0:T(2,128)} %bitcast.7, bf16[8,128,128]{2,1,0:T(8,128)(2,1)} %bitcast.6, bf16[128,128,128]{2,1,0:T(8,128)(2,1)} %bitcast.5), custom_call_target="tpu_custom_call" | custom-call | tf_op jit(solution)/shard_map/pallas_call | solution.py:437
  47.6 1.7 %shard_map.78 = (f32[256,128]{1,0:T(8,128)}, f32[256,128]{1,0:T(8,128)}) custom-call(f32[256,128]{1,0:T(8,128)} %get-tuple-element.4.x_ref, f32[256,128]{1,0:T(8,128)} %get-tuple-element.5.r_ref), custom_call_target="tpu_custom_call" | custom-call | tf_op jit(solution)/shard_map/pallas_call | solution.py:510

commit v4 on v3

--- a/solution.py
+++ b/solution.py
@@ -8,7 +8,7 @@
 from jax.sharding import PartitionSpec as P
 
 ITERS = 2
-CHUNKS = 4
+CHUNKS = 2
 LAG = 3
 
 reg_weight = 0.0004
@@ -376,7 +376,7 @@
             pcur[u] = direction.astype(jnp.bfloat16)
 
     order = sorted(range(cols), key=lambda c: (-abs(2 * c - cols + 1), c))
-    order = [c * own_users + j for c in order for j in range(own_users)]
+    order = [c * own_users + j for j in range(own_users) for c in order]
     for u in order:
         @pl.when(my_col != u // own_users)
         def _():

time: 49.5 us -> 48.9 us (0.988)
  Pallas kernels: 48.7 us -> 48.1 us
    pallas_call x1, Pallas kernels: 47 us -> 46.4 us  [per_device(): pl.pallas_call(functools.partial(sweep_kernel, sizes), out_shape=(jax.Sha...]
where the time goes in v4:
time: 48.9 us; the launch traced here: 48.7 us
  Pallas kernels  48.1 us (98%)
  between operations  0.64 us (1%)
    pallas_call x1, Pallas kernels, per_device(): pl.pallas_call(functools.partial(sweep_kernel, sizes), out_shape=(jax.Sha...  46.4 us
    pallas_call x1, Pallas kernels, hand_out(): pl.pallas_call(tail_kernel, out_shape=(jax.ShapeDtypeStruct(x.shape, x.dt...  1.68 us

profile of v4, /device:TPU:0, one launch (start us, length us, event | category | flops | bytes accessed | tf_op | source)
XLA Modules:
  0.0 48.7 jit_solution(7493888518292818954)
XLA Ops:
  0.6 46.4 %shard_map.77 = (f32[256,128]{1,0:T(8,128)}, f32[256,128]{1,0:T(8,128)}) custom-call(s32[1,128]{1,0:T(1,128)} %bitcast.8, s32[1,128]{1,0:T(1,128)} %bitcast.9, f32[256,128]{1,0:T(8,128)} %uf_hbm.1, s32[2,128]{1,0:T(2,128)} %bitcast.7, bf16[8,128,128]{2,1,0:T(8,128)(2,1)} %bitcast.6, bf16[128,128,128]{2,1,0:T(8,128)(2,1)} %bitcast.5), custom_call_target="tpu_custom_call" | custom-call | tf_op jit(solution)/shard_map/pallas_call | solution.py:437
  47.0 1.7 %shard_map.78 = (f32[256,128]{1,0:T(8,128)}, f32[256,128]{1,0:T(8,128)}) custom-call(f32[256,128]{1,0:T(8,128)} %get-tuple-element.4.x_ref, f32[256,128]{1,0:T(8,128)} %get-tuple-element.5.r_ref), custom_call_target="tpu_custom_call" | custom-call | tf_op jit(solution)/shard_map/pallas_call | solution.py:510

commit v5 on v4

--- a/solution.py
+++ b/solution.py
@@ -10,6 +10,7 @@
 ITERS = 2
 CHUNKS = 2
 LAG = 3
+CUTS = 1
 
 reg_weight = 0.0004
 tiny = 1e-06
@@ -47,7 +48,7 @@
 
 def sweep_kernel(
     sizes, owner_hbm, column_hbm, uf_hbm, counts_hbm, items_hbm, ratings_hbm, x_ref, r_ref,
-    vbuf, rbuf, start, pcur, part, sent, recv, tot, last, p_ref, res_ref, xacc, damp_ref, counts_ref,
+    vbuf, rbuf, start, pcur, part, sent, recv, tot, leaving, last, p_ref, res_ref, xacc, damp_ref, counts_ref,
     ids, places, pos_ref, user_sem, count_sem, id_sem, place_sem, item_sem, rating_sem, i_send, i_recv,
     v_send, v_recv, d_send, d_recv, t_send, t_recv,
     g_send, g_recv, in_send, in_recv, out_send, f_send, f_recv,
@@ -259,32 +260,34 @@
     for copy in rating_sends + shared:
         copy.wait_recv()
 
-    def inward(stage, u):
+    cut_rows = block // CUTS
+
+    def inward(stage, u, h):
         return pltpu.make_async_remote_copy(
-            src_ref=sent.at[stage, u],
-            dst_ref=recv.at[side, stage, u],
-            send_sem=in_send.at[stage, u],
-            recv_sem=in_recv.at[side, stage, u],
+            src_ref=sent.at[stage, u, h],
+            dst_ref=recv.at[side, stage, u, h],
+            send_sem=in_send.at[stage, u, h],
+            recv_sem=in_recv.at[side, stage, u, h],
             device_id={"col": inner},
             device_id_type=MESH,
         )
 
-    def outward(stage, u):
+    def outward(stage, u, h):
         return pltpu.make_async_remote_copy(
-            src_ref=tot.at[stage, u],
-            dst_ref=recv.at[1, stage, u],
-            send_sem=out_send.at[stage, u],
-            recv_sem=in_recv.at[1, stage, u],
+            src_ref=tot.at[stage, u, h],
+            dst_ref=recv.at[1, stage, u, h],
+            send_sem=out_send.at[stage, u, h],
+            recv_sem=in_recv.at[1, stage, u, h],
             device_id={"col": outer},
             device_id_type=MESH,
         )
 
-    def arrival(which, stage, u):
+    def arrival(which, stage, u, h):
         return pltpu.make_async_remote_copy(
-            src_ref=sent.at[stage, u],
-            dst_ref=recv.at[which, stage, u],
-            send_sem=in_send.at[stage, u],
-            recv_sem=in_recv.at[which, stage, u],
+            src_ref=sent.at[stage, u, h],
+            dst_ref=recv.at[which, stage, u, h],
+            send_sem=in_send.at[stage, u, h],
+            recv_sem=in_recv.at[which, stage, u, h],
             device_id={"col": inner},
             device_id_type=MESH,
         )
@@ -309,7 +312,7 @@
 
     def deliver(d, j, target, source):
         return pltpu.make_async_remote_copy(
-            src_ref=sent.at[ITERS, target * own_users + j],
+            src_ref=leaving.at[target * own_users + j],
             dst_ref=last.at[source, j],
             send_sem=f_send.at[d, j],
             recv_sem=f_recv.at[source, j],
@@ -322,41 +325,49 @@
         if stage == ITERS:
             @pl.when(my_col != u // own_users)
             def _():
-                store_coded(sent, (stage, u), part[u])
+                store_coded(leaving, (u,), part[u])
                 deliver(u // own_users, u % own_users, u // own_users, my_col).start()
 
             return
 
         @pl.when(depth == 0)
         def _():
-            store_coded(sent, (stage, u), part[u])
-            inward(stage, u).start()
+            for h in range(CUTS):
+                store_coded(sent, (stage, u, h), part[u, pl.ds(h * cut_rows, cut_rows)])
+                inward(stage, u, h).start()
 
     def pass_on(stage, u):
         @pl.when(depth > 0)
         def _():
-            arrival(0, stage, u).wait_recv()
-            store_coded(sent, (stage, u), part[u] + load_coded(recv, (0, stage, u)))
-            inward(stage, u).start()
+            for h in range(CUTS):
+                arrival(0, stage, u, h).wait_recv()
+                mine = part[u, pl.ds(h * cut_rows, cut_rows)]
+                store_coded(sent, (stage, u, h), mine + load_coded(recv, (0, stage, u, h)))
+                inward(stage, u, h).start()
 
     def collect(stage, u):
-        arrival(1, stage, u).wait_recv()
-
         @pl.when(depth == half - 1)
         def _():
-            store_coded(tot, (stage, u), load_coded(sent, (stage, u)) + load_coded(recv, (1, stage, u)))
+            for h in range(CUTS):
+                arrival(1, stage, u, h).wait_recv()
+                both = load_coded(sent, (stage, u, h)) + load_coded(recv, (1, stage, u, h))
+                store_coded(tot, (stage, u, h), both)
+                if half > 1:
+                    outward(stage, u, h).start()
 
         @pl.when(depth < half - 1)
         def _():
-            tot[stage, u] = recv[1, stage, u]
-
-        @pl.when(depth > 0)
-        def _():
-            outward(stage, u).start()
+            for h in range(CUTS):
+                arrival(1, stage, u, h).wait_recv()
+                tot[stage, u, h] = recv[1, stage, u, h]
+
+                @pl.when(depth > 0)
+                def _():
+                    outward(stage, u, h).start()
 
     def update(stage, u, image=None):
         if stage < ITERS:
-            image = load_coded(tot, (stage, u))
+            image = jnp.concatenate([load_coded(tot, (stage, u, h)) for h in range(CUTS)], axis=0)
         if stage == 0:
             res_ref[u] = image
             p_ref[u] = image
@@ -412,13 +423,15 @@
             deliver(col_of(d), j, col_of(d), my_col).wait_send()
     for stage in range(ITERS):
         for u in order:
-            inward(stage, u).wait_send()
+            for h in range(CUTS):
+                inward(stage, u, h).wait_send()
 
     @pl.when(depth > 0)
     def _():
         for stage in range(ITERS):
             for u in order:
-                outward(stage, u).wait_send()
+                for h in range(CUTS):
+                    outward(stage, u, h).wait_send()
 
 
 def per_device(sizes, user_factors, item_factors, ratings, block_user, block_item, counts):
@@ -429,7 +442,6 @@
     own_users = users // block
     item_blocks = item_factors.shape[0] // block
 
-    stages = ITERS + 1
     slots = cols * own_users
     dma = pltpu.SemaphoreType.DMA
     vmem = pl.BlockSpec(memory_space=pltpu.VMEM)
@@ -448,9 +460,10 @@
             pltpu.VMEM((slots, block, rank), jnp.bfloat16),
             pltpu.VMEM((slots, block, rank), jnp.bfloat16),
             pltpu.VMEM((slots, block, rank), jnp.float32),
-            pltpu.VMEM((stages, slots, block + pad, rank), jnp.int16),
-            pltpu.VMEM((2, ITERS, slots, block + pad, rank), jnp.int16),
-            pltpu.VMEM((ITERS, slots, block + pad, rank), jnp.int16),
+            pltpu.VMEM((ITERS, slots, CUTS, block // CUTS + pad, rank), jnp.int16),
+            pltpu.VMEM((2, ITERS, slots, CUTS, block // CUTS + pad, rank), jnp.int16),
+            pltpu.VMEM((ITERS, slots, CUTS, block // CUTS + pad, rank), jnp.int16),
+            pltpu.VMEM((slots, block + pad, rank), jnp.int16),
             pltpu.VMEM((cols, own_users, block + pad, rank), jnp.int16),
             pltpu.VMEM((slots, block, rank), jnp.float32),
             pltpu.VMEM((slots, block, rank), jnp.float32),
@@ -476,9 +489,9 @@
             dma((fibers, CHUNKS)),
             dma((cols, own_users)),
             dma((slots,)),
-            dma((ITERS, slots)),
-            dma((2, ITERS, slots)),
-            dma((ITERS, slots)),
+            dma((ITERS, slots, CUTS)),
+            dma((2, ITERS, slots, CUTS)),
+            dma((ITERS, slots, CUTS)),
             dma((cols, own_users)),
             dma((cols, own_users)),
         ],

time: 48.9 us -> 48.8 us (level)
  no operation moved by 1% of the time
where the time goes in v5:
time: 48.8 us; the launch traced here: 48.7 us
  Pallas kernels  48.1 us (99%)
  between operations  0.64 us (1%)
    pallas_call x1, Pallas kernels, per_device(): pl.pallas_call(functools.partial(sweep_kernel, sizes), out_shape=(jax.Sha...  46.4 us
    pallas_call x1, Pallas kernels, hand_out(): pl.pallas_call(tail_kernel, out_shape=(jax.ShapeDtypeStruct(x.shape, x.dt...  1.68 us

profile of v5, /device:TPU:0, one launch (start us, length us, event | category | flops | bytes accessed | tf_op | source)
XLA Modules:
  0.0 48.7 jit_solution(5674504124272693929)
XLA Ops:
  0.6 46.4 %shard_map.77 = (f32[256,128]{1,0:T(8,128)}, f32[256,128]{1,0:T(8,128)}) custom-call(s32[1,128]{1,0:T(1,128)} %bitcast.8, s32[1,128]{1,0:T(1,128)} %bitcast.9, f32[256,128]{1,0:T(8,128)} %uf_hbm.1, s32[2,128]{1,0:T(2,128)} %bitcast.7, bf16[8,128,128]{2,1,0:T(8,128)(2,1)} %bitcast.6, bf16[128,128,128]{2,1,0:T(8,128)(2,1)} %bitcast.5), custom_call_target="tpu_custom_call" | custom-call | tf_op jit(solution)/shard_map/pallas_call | solution.py:449
  47.0 1.7 %shard_map.78 = (f32[256,128]{1,0:T(8,128)}, f32[256,128]{1,0:T(8,128)}) custom-call(f32[256,128]{1,0:T(8,128)} %get-tuple-element.4.x_ref, f32[256,128]{1,0:T(8,128)} %get-tuple-element.5.r_ref), custom_call_target="tpu_custom_call" | custom-call | tf_op jit(solution)/shard_map/pallas_call | solution.py:523
